TPU v7x, 8 devices: a whole 2x2x1 slice. The times are simulated.
8 devices in a mesh: rep: 1 (over z), dp: 8 (over x, y, core).
Axes of the slice: x: 2, y: 2, z: 1, core: 2. Of those that a mesh axis runs over, the one named last changes fastest.
Arguments:
- a: bfloat16 [8, 4, 4096, 1024], P(('rep', 'dp'))
- g: bfloat16 [8, 4, 4096, 3328], P(('rep', 'dp'))
Outputs:
- output: bfloat16 [4, 1024, 3328], P('rep')
All inputs are finite; a program needn't handle non-finite values.
Results may differ from a plain program's by a relative error of at most 0.012.
Values are sent between devices in bfloat16 or wider.
A program may use at most 2 GiB of HBM per device.

v0:
```python
import jax
import jax.numpy as jnp


def solution(mesh):
    groups = mesh.shape["rep"]

    def step(a, g):
        a, g = (t.reshape(groups, -1, *t.shape[1:]) for t in (a, g))
        sums = jnp.einsum("rsntd,rsntf->rndf", a, g, preferred_element_type=jnp.float32)
        return sums.astype(jnp.bfloat16).reshape(-1, *sums.shape[2:])

    return step
```

profile of v0, /device:TPU:0, one launch (start us, length us, event | category | flops | bytes accessed | tf_op | source)
XLA Modules:
  0.0 763.3 jit_solution(7034331158191032012)
XLA Ops:
  0.0 129.7 %fusion = f32[4,1024,3328]{2,1,0:T(8,128)} fusion(bf16[1,4,4096,3328]{3,2,1,0:T(8,128)(2,1)} %param.1, bf16[1,4,4096,1024]{3,2,1,0:T(8,128)(2,1)} %param), kind=kOutput, calls=%fused_computation | convolution fusion | flops 111669149696 | bytes 197132288 | tf_op jit(solution)/rsntd,rsntf->rndf/dot_general | solution.py:10
  129.7 633.6 %all-reduce.2 = bf16[4,1024,3328]{2,1,0:T(8,128)(2,1)} all-reduce(f32[4,1024,3328]{2,1,0:T(8,128)} %fusion), channel_id=1, replica_groups=mesh['axis_0'=8] {'axis_0'}, use_global_device_ids=true, to_apply=%add.clone | all-reduce | flops 13631488 | bytes 81788928 | tf_op jit(solution)/rsntd,rsntf->rndf/dot_general | solution.py:10
where the time goes:
time: 763 us
  blocking collectives  634 us (83%)
  matrix products  130 us (17%)
    dot_general x1, blocking collectives, step(): jnp.einsum('rsntd,rsntf->rndf', a, g, preferred_element_type=jnp.float32)  634 us
    dot_general x1, matrix products, step(): jnp.einsum('rsntd,rsntf->rndf', a, g, preferred_element_type=jnp.float32)  130 us

commit v1 on v0

v1 whole, which is shorter than its diff:
```python
import functools
import jax
import jax.numpy as jnp
from jax import lax
from jax.experimental import pallas as pl
from jax.experimental.pallas import tpu as pltpu
from jax.sharding import PartitionSpec as P

MESH = pl.DeviceIdType.MESH
W = 256
KC = 512
AG_START, AG_EVERY = 8, 4


def kernel(a_ref, g_ref, t_ref, at, a_in, g_in, mine, d2d_out, d2d_got, rs1_out, rs1_got, keep1,
           rs2_out, rs2_got, keep2, fin,
           a_sem, g_sem, d2d_s, d2d_r, rs1_s, rs1_r, rs2_s, rs2_r, ag1_r, ag2a_r, ag2b_r, sib_r, ag_s, loc_s):
    mats, tokens, d = a_ref.shape[1:]
    ff = g_ref.shape[3]
    nb = ff // W
    rounds = mats * nb
    half_d, h, q4 = d // 2, d // 4, d // 8
    chunks = tokens // KC

    me = lax.axis_index("dp")
    x, y, c = me // 4, (me // 2) % 2, me % 2
    pa = (1 - c) * x + c * y
    pb = (1 - c) * y + c * x
    to_a = me + (1 - c) * (4 - 8 * x) + c * (2 - 4 * y)
    to_b = me + (1 - c) * (2 - 4 * y) + c * (4 - 8 * x)
    sib = me + 1 - 2 * c
    own, other = half_d * c, half_d * (1 - c)

    def at_rows(ref, start, size):
        return ref.at[pl.ds(pl.multiple_of(start, 128), size)]

    def remote(src, dst, s, r, dev):
        return pltpu.make_async_remote_copy(src_ref=src, dst_ref=dst, send_sem=s, recv_sem=r,
                                            device_id={"dp": dev}, device_id_type=MESH)

    def tile(r, start, size):
        n, j = r // nb, r % nb
        return t_ref.at[n, pl.ds(pl.multiple_of(start, 128), size), pl.ds(pl.multiple_of(j * W, W), W)]

    def g_copy(r):
        n, j = r // nb, r % nb
        return pltpu.make_async_copy(g_ref.at[0, n, :, pl.ds(pl.multiple_of(j * W, W), W)],
                                     g_in.at[r % 3], g_sem.at[r % 3])

    def a_copy(n, k):
        return pltpu.make_async_copy(a_ref.at[0, n, pl.ds(pl.multiple_of(k * KC, KC), KC)],
                                     a_in.at[k % 2], a_sem.at[k % 2])

    def turn(n, k):
        at[n % 2, :, pl.ds(pl.multiple_of(k * KC, KC), KC)] = a_in[k % 2].T

    def d2d(r):
        return remote(d2d_out.at[r % 4], d2d_got.at[r % 4], d2d_s.at[r % 4], d2d_r.at[r % 4], sib)

    def rs1(r):
        return remote(rs1_out.at[r % 8], rs1_got.at[r % 8], rs1_s.at[r % 8], rs1_r.at[r % 8], to_a)

    def rs2(r):
        return remote(rs2_out.at[r % 8], rs2_got.at[r % 8], rs2_s.at[r % 8], rs2_r.at[r % 8], to_b)

    def dot(r, rows):
        return jnp.dot(at[(r // nb) % 2, pl.ds(pl.multiple_of(rows, half_d), half_d), :], g_in[r % 3],
                       preferred_element_type=jnp.float32)

    def combine(r):
        d2d(r).wait_recv()
        lo, up = pl.multiple_of(h * (1 - pa), h), pl.multiple_of(h * pa, h)

        @pl.when(r >= 8)
        def _():
            rs1(r - 8).wait_send()

        rs1_out[r % 8] = (mine[pl.ds(lo, h)] + d2d_got[r % 4, pl.ds(lo, h)].astype(jnp.float32)).astype(jnp.bfloat16)
        rs1(r).start()
        keep1[r % 4] = mine[pl.ds(up, h)] + d2d_got[r % 4, pl.ds(up, h)].astype(jnp.float32)

    def stage2(r):
        rs1(r).wait_recv()
        lo, up = pl.multiple_of(q4 * (1 - pb), q4), pl.multiple_of(q4 * pb, q4)

        @pl.when(r >= 8)
        def _():
            rs2(r - 8).wait_send()

        rs2_out[r % 8] = (keep1[r % 4, pl.ds(lo, q4)] + rs1_got[r % 8, pl.ds(lo, q4)].astype(jnp.float32)).astype(jnp.bfloat16)
        rs2(r).start()
        keep2[r % 4] = keep1[r % 4, pl.ds(up, q4)] + rs1_got[r % 8, pl.ds(up, q4)].astype(jnp.float32)

    def stage3(r):
        rs2(r).wait_recv()
        fin[r] = (keep2[r % 4] + rs2_got[r % 8].astype(jnp.float32)).astype(jnp.bfloat16)

    def quarter(p, q):
        return own + h * p + q4 * q

    def spread1(r):
        dst = tile(r, quarter(pa, pb), q4)
        remote(fin.at[r], dst, ag_s, ag1_r.at[r], to_b).start()
        remote(fin.at[r], dst, ag_s, ag2a_r.at[r], to_a).start()
        remote(fin.at[r], dst, ag_s, sib_r, sib).start()
        pltpu.make_async_copy(fin.at[r], dst, loc_s).start()

    def spread2(r):
        src = tile(r, quarter(pa, 1 - pb), q4)
        remote(fin.at[r], src, ag_s, ag1_r.at[r], to_b).wait_recv()
        remote(src, src, ag_s, ag2b_r.at[r], to_a).start()
        remote(src, src, ag_s, sib_r, sib).start()

    def spread3(r):
        dst = tile(r, quarter(1 - pa, pb), q4)
        remote(fin.at[r], dst, ag_s, ag2a_r.at[r], to_a).wait_recv()
        dst = tile(r, quarter(1 - pa, 1 - pb), q4)
        remote(fin.at[r], dst, ag_s, ag2b_r.at[r], to_a).wait_recv()
        src = tile(r, own + h * (1 - pa), h)
        remote(src, src, ag_s, sib_r, sib).start()

    a_copy(0, 0).start()
    a_copy(0, 1).start()
    for r in range(2):
        g_copy(r).start()

    barrier = pltpu.get_barrier_semaphore()
    for dev in (sib, to_a, to_b):
        pl.semaphore_signal(barrier, inc=1, device_id={"dp": dev}, device_id_type=MESH)
    pl.semaphore_wait(barrier, 3)

    @pl.loop(0, chunks)
    def _(k):
        a_copy(0, k).wait()
        turn(0, k)

        @pl.when(k + 2 < chunks)
        def _():
            a_copy(0, k + 2).start()

    @pl.loop(0, rounds + 5)
    def _(r):
        n, j = r // nb, r % nb
        nxt = (n + 1 < mats)

        @pl.when(r < rounds)
        def _():
            @pl.when(nxt & (j == 0))
            def _():
                a_copy(n + 1, 0).start()
                a_copy(n + 1, 1).start()

            g_copy(r).wait()

            @pl.when(r + 2 < rounds)
            def _():
                g_copy(r + 2).start()

            @pl.when(r >= 4)
            def _():
                d2d(r - 4).wait_send()

            d2d_out[r % 4] = dot(r, other).astype(jnp.bfloat16)
            d2d(r).start()

        @pl.when((r >= 1) & (r <= rounds))
        def _():
            combine(r - 1)

        @pl.when(r < rounds)
        def _():
            mine[...] = dot(r, own)

        @pl.when((r >= 3) & (r < rounds + 3))
        def _():
            stage2(r - 3)

        @pl.when(r >= 5)
        def _():
            stage3(r - 5)

        @pl.when(nxt & (j >= 1) & (j <= chunks))
        def _():
            k = j - 1
            a_copy(n + 1, k).wait()
            turn(n + 1, k)

            @pl.when(k + 2 < chunks)
            def _():
                a_copy(n + 1, k + 2).start()

        s = (r - AG_START) // AG_EVERY

        @pl.when((r >= AG_START) & ((r - AG_START) % AG_EVERY == 0))
        def _():
            spread1(s)

            @pl.when(s >= 1)
            def _():
                spread2(s - 1)

            @pl.when(s >= 2)
            def _():
                spread3(s - 2)

    done = (rounds + 5 - AG_START + AG_EVERY - 1) // AG_EVERY

    @pl.loop(done, rounds)
    def _(s):
        spread1(s)

    @pl.loop(done - 1, rounds + 1)
    def _(s):
        @pl.when(s < rounds)
        def _():
            spread2(s)

        spread3(s - 1)

    for k in range(4):
        d2d(rounds - 4 + k).wait_send()
    for k in range(8):
        rs1(rounds - 8 + k).wait_send()
        rs2(rounds - 8 + k).wait_send()
    whole = t_ref.at[:, pl.ds(0, d - q4), :]
    remote(whole, whole, ag_s, sib_r, sib).wait_send()
    part = t_ref.at[:, pl.ds(0, half_d), :]
    remote(part, part, ag_s, sib_r, sib).wait_recv()
    mini = t_ref.at[:, pl.ds(0, q4), :]
    pltpu.make_async_copy(mini, mini, loc_s).wait()


def solution(mesh):
    def step(a, g):
        mats, tokens, d = a.shape[1:]
        ff = g.shape[3]
        rounds = mats * (ff // W)
        bf, f32 = jnp.bfloat16, jnp.float32
        dma = pltpu.SemaphoreType.DMA
        scratch = [
            pltpu.VMEM((2, d, tokens), bf),
            pltpu.VMEM((2, KC, d), bf),
            pltpu.VMEM((3, tokens, W), bf),
            pltpu.VMEM((d // 2, W), f32),
            pltpu.VMEM((4, d // 2, W), bf),
            pltpu.VMEM((4, d // 2, W), bf),
            pltpu.VMEM((8, d // 4, W), bf),
            pltpu.VMEM((8, d // 4, W), bf),
            pltpu.VMEM((4, d // 4, W), f32),
            pltpu.VMEM((8, d // 8, W), bf),
            pltpu.VMEM((8, d // 8, W), bf),
            pltpu.VMEM((4, d // 8, W), f32),
            pltpu.VMEM((rounds, d // 8, W), bf),
            dma((2,)), dma((3,)), dma((4,)), dma((4,)), dma((8,)), dma((8,)), dma((8,)), dma((8,)),
            dma((rounds,)), dma((rounds,)), dma((rounds,)), dma, dma, dma,
        ]
        return pl.pallas_call(
            kernel,
            out_shape=jax.ShapeDtypeStruct((mats, d, ff), bf),
            in_specs=[pl.BlockSpec(memory_space=pl.ANY)] * 2,
            out_specs=pl.BlockSpec(memory_space=pl.ANY),
            scratch_shapes=scratch,
            compiler_params=pltpu.CompilerParams(collective_id=0, has_side_effects=True, vmem_limit_bytes=60 << 20),
            name="sums",
        )(a, g)

    return jax.shard_map(step, mesh=mesh, in_specs=(P(("rep", "dp")), P(("rep", "dp"))), out_specs=P("rep"),
                         check_vma=False)
```

time: 763 us -> 313 us (0.41)
  blocking collectives: 634 us -> 0 us
  Pallas kernels: 0 us -> 293 us
  matrix products: 130 us -> 0 us
  local copies, waits for them, and re-layouts: 0 us -> 19.3 us
    dot_general x1 -> x0, blocking collectives: 634 us -> none  [step(): jnp.einsum('rsntd,rsntf->rndf', a, g, preferred_element_type=jnp.float32)]
    pallas_call x0 -> x1, Pallas kernels: none -> 293 us  [step(): pl.pallas_call(kernel, out_shape=jax.ShapeDtypeStruct((mats, d, ff), bf),...]
    dot_general x1 -> x0, matrix products: 130 us -> none  [step(): jnp.einsum('rsntd,rsntf->rndf', a, g, preferred_element_type=jnp.float32)]
    unnamed x0 -> x1, local copies, waits for them, and re-layouts: none -> 19.3 us
where the time goes in v1:
time: 313 us
  Pallas kernels  293 us (94%)
  local copies, waits for them, and re-layouts  19.3 us (6%)
    pallas_call x1, Pallas kernels, step(): pl.pallas_call(kernel, out_shape=jax.ShapeDtypeStruct((mats, d, ff), bf),...  293 us
    unnamed x1, local copies, waits for them, and re-layouts  19.3 us

profile of v1, /device:TPU:0, one launch (start us, length us, event | category | flops | bytes accessed | tf_op | source)
XLA Modules:
  0.0 312.5 jit_solution(151899279106507844)
XLA Ops:
  0.0 293.2 %sums.1 = bf16[4,1024,3328]{2,1,0:T(8,128)(2,1)} custom-call(bf16[1,4,4096,1024]{3,2,1,0:T(8,128)(2,1)} %a_ref.1, bf16[1,4,4096,3328]{3,2,1,0:T(8,128)(2,1)} %g_ref.1), custom_call_target="tpu_custom_call" | custom-call | tf_op jit(solution)/shard_map/sums/pallas_call | solution.py:257
  293.2 19.3 %copy.4 = bf16[4,1024,3328]{2,1,0:T(8,128)(2,1)} copy(bf16[4,1024,3328]{2,1,0:T(8,128)(2,1)} %sums.1) | data formatting | bytes 54525952

commit v2 on v0

v2 whole, which is shorter than its diff:
```python
import jax
import jax.numpy as jnp
from jax import lax
from jax.experimental import pallas as pl
from jax.experimental.pallas import tpu as pltpu
from jax.sharding import PartitionSpec as P

MESH = pl.DeviceIdType.MESH
W = 256
LAG1, LAG2, LAG3 = 1, 3, 5
AG_START, AG_EVERY = 7, 1


def kernel(a_ref, g_ref, t_ref, a_in, g_in, mine, d2d_out, d2d_got, rs1_out, rs1_got, keep1,
           rs2_out, rs2_got, keep2,
           a_sem, g_sem, d2d_s, d2d_r, rs1_s, rs1_r, rs2_s, rs2_r, ag1_r, ag2a_r, ag2b_r, sib_r, ag_s):
    mats, tokens, d = a_ref.shape[1:]
    ff = g_ref.shape[3]
    nb = ff // W
    rounds = mats * nb
    half_d, h, q4 = d // 2, d // 4, d // 8
    f32, bf = jnp.float32, jnp.bfloat16

    me = lax.axis_index("dp")
    x, y, c = me // 4, (me // 2) % 2, me % 2
    pa = (1 - c) * x + c * y
    pb = (1 - c) * y + c * x
    to_a = me + (1 - c) * (4 - 8 * x) + c * (2 - 4 * y)
    to_b = me + (1 - c) * (2 - 4 * y) + c * (4 - 8 * x)
    sib = me + 1 - 2 * c
    own, other = half_d * c, half_d * (1 - c)

    def remote(src, dst, s, r, dev):
        return pltpu.make_async_remote_copy(src_ref=src, dst_ref=dst, send_sem=s, recv_sem=r,
                                            device_id={"dp": dev}, device_id_type=MESH)

    def cut(r, start, size):
        return r // nb, pl.ds(pl.multiple_of(start, 128), size), pl.ds(pl.multiple_of((r % nb) * W, W), W)

    def tile(r, start, size):
        return t_ref.at[cut(r, start, size)]

    def g_copy(r):
        return pltpu.make_async_copy(g_ref.at[0, r // nb, :, pl.ds(pl.multiple_of((r % nb) * W, W), W)],
                                     g_in.at[r % 3], g_sem.at[r % 3])

    def a_copy(n, i):
        cols = pl.ds(half_d * i, half_d)
        return pltpu.make_async_copy(a_ref.at[0, n, :, cols], a_in.at[n % 2, i], a_sem.at[n % 2, i])

    def a_side(n, side):
        cols = pl.ds(pl.multiple_of(side, half_d), half_d)
        return pltpu.make_async_copy(a_ref.at[0, n, :, cols], a_in.at[n % 2, side // half_d],
                                     a_sem.at[n % 2, side // half_d])

    def d2d(r):
        return remote(d2d_out.at[r % 4], d2d_got.at[r % 4], d2d_s.at[r % 4], d2d_r.at[r % 4], sib)

    def rs1(r):
        return remote(rs1_out.at[r % 8], rs1_got.at[r % 8], rs1_s.at[r % 8], rs1_r.at[r % 8], to_a)

    def rs2(r):
        return remote(rs2_out.at[r % 8], rs2_got.at[r % 8], rs2_s.at[r % 8], rs2_r.at[r % 8], to_b)

    def dot(r, side):
        return lax.dot_general(a_in[(r // nb) % 2, side // half_d], g_in[r % 3],
                               (((0,), (0,)), ((), ())), preferred_element_type=f32)

    def combine(r):
        lo, up = pl.multiple_of(h * (1 - pa), h), pl.multiple_of(h * pa, h)
        rs1_out[r % 8] = (mine[r % 2, pl.ds(lo, h)] + d2d_got[r % 4, pl.ds(lo, h)].astype(f32)).astype(bf)
        keep1[r % 4] = mine[r % 2, pl.ds(up, h)] + d2d_got[r % 4, pl.ds(up, h)].astype(f32)

    def stage2(r):
        lo, up = pl.multiple_of(q4 * (1 - pb), q4), pl.multiple_of(q4 * pb, q4)
        rs2_out[r % 8] = (keep1[r % 4, pl.ds(lo, q4)] + rs1_got[r % 8, pl.ds(lo, q4)].astype(f32)).astype(bf)
        keep2[r % 4] = keep1[r % 4, pl.ds(up, q4)] + rs1_got[r % 8, pl.ds(up, q4)].astype(f32)

    def quarter(p, q):
        return own + h * p + q4 * q

    def stage3(r):
        t_ref[cut(r, quarter(pa, pb), q4)] = (keep2[r % 4] + rs2_got[r % 8].astype(f32)).astype(bf)

    def spread1(r):
        src = tile(r, quarter(pa, pb), q4)
        remote(src, src, ag_s, ag1_r.at[r], to_b).start()
        remote(src, src, ag_s, ag2a_r.at[r], to_a).start()
        remote(src, src, ag_s, sib_r, sib).start()

    def spread2(r):
        src = tile(r, quarter(pa, 1 - pb), q4)
        remote(src, src, ag_s, ag1_r.at[r], to_b).wait_recv()
        remote(src, src, ag_s, ag2b_r.at[r], to_a).start()
        remote(src, src, ag_s, sib_r, sib).start()

    def spread3(r):
        dst = tile(r, quarter(1 - pa, pb), q4)
        remote(dst, dst, ag_s, ag2a_r.at[r], to_a).wait_recv()
        dst = tile(r, quarter(1 - pa, 1 - pb), q4)
        remote(dst, dst, ag_s, ag2b_r.at[r], to_a).wait_recv()
        src = tile(r, own + h * (1 - pa), h)
        remote(src, src, ag_s, sib_r, sib).start()

    def when(cond, f):
        if cond is True:
            f()
        elif cond is not False:
            pl.when(cond)(f)

    def both(p, q):
        return q if p is True else p & q

    def spread(r):
        s = (r - AG_START) // AG_EVERY

        @pl.when((r >= AG_START) & ((r - AG_START) % AG_EVERY == 0))
        def _():
            spread1(s)

            @pl.when(s >= 1)
            def _():
                spread2(s - 1)

            @pl.when(s >= 2)
            def _():
                spread3(s - 2)

    def round_(r, first=False, compute=True, one=True, two=True, three=True, reuse=True):
        if compute:
            n, j = r // nb, r % nb

            @pl.when((j == 2) & (n + 1 < mats))
            def _():
                for i in range(2):
                    a_copy(n + 1, i).start()

            @pl.when((j == 0) & (n > 0))
            def _():
                for i in range(2):
                    a_copy(n, i).wait()

            g_copy(r).wait()

            @pl.when(r + 2 < rounds)
            def _():
                g_copy(r + 2).start()

            if first:
                @pl.when(r == 0)
                def _():
                    a_side(0, other).wait()
            when((r >= 4) if first else True, lambda: d2d(r - 4).wait_send())
            @pl.when(me >= 0)
            def _():
                d2d_out[r % 4] = dot(r, other).astype(bf)

            d2d(r).start()
            if first:
                @pl.when(r == 0)
                def _():
                    a_side(0, own).wait()

        when(one, lambda: d2d(r - LAG1).wait_recv())
        when(two, lambda: rs1(r - LAG2).wait_recv())
        when(three, lambda: rs2(r - LAG3).wait_recv())
        when(both(one, r - LAG1 >= 8), lambda: rs1(r - LAG1 - 8).wait_send())
        when(both(two, r - LAG2 >= 8), lambda: rs2(r - LAG2 - 8).wait_send())
        when(one, lambda: combine(r - LAG1))
        when(one, lambda: rs1(r - LAG1).start())
        when(two, lambda: stage2(r - LAG2))
        when(two, lambda: rs2(r - LAG2).start())
        if compute:
            mine[r % 2] = dot(r, own)
        when(three, lambda: stage3(r - LAG3))
        spread(r)

    a_side(0, other).start()
    g_copy(0).start()
    a_side(0, own).start()
    g_copy(1).start()

    barrier = pltpu.get_barrier_semaphore()
    for dev in (sib, to_a, to_b):
        pl.semaphore_signal(barrier, inc=1, device_id={"dp": dev}, device_id_type=MESH)
    pl.semaphore_wait(barrier, 3)

    @pl.loop(0, LAG3)
    def _(r):
        round_(r, first=True, one=r >= LAG1, two=r >= LAG2, three=False)

    @pl.loop(LAG3, rounds)
    def _(r):
        round_(r)

    @pl.loop(rounds, rounds + LAG3)
    def _(r):
        round_(r, compute=False, one=r < rounds + LAG1, two=r < rounds + LAG2)

    done = -(-(rounds + LAG3 - AG_START) // AG_EVERY)

    @pl.loop(done, rounds)
    def _(s):
        spread1(s)

    @pl.loop(done - 1, rounds + 1)
    def _(s):
        @pl.when(s < rounds)
        def _():
            spread2(s)

        spread3(s - 1)

    for k in range(4):
        d2d(rounds - 4 + k).wait_send()
    for k in range(8):
        rs1(rounds - 8 + k).wait_send()
        rs2(rounds - 8 + k).wait_send()
    whole = t_ref.at[:, pl.ds(0, d - q4), :]
    remote(whole, whole, ag_s, sib_r, sib).wait_send()
    part = t_ref.at[:, pl.ds(0, half_d), :]
    remote(part, part, ag_s, sib_r, sib).wait_recv()


def put(t_ref, o_ref, sem):
    copies = [pltpu.make_async_copy(t_ref.at[n], o_ref.at[n], sem.at[n]) for n in range(t_ref.shape[0])]
    for copy in copies:
        copy.start()
    for copy in copies:
        copy.wait()


def solution(mesh):
    def step(a, g):
        mats, tokens, d = a.shape[1:]
        ff = g.shape[3]
        rounds = mats * (ff // W)
        bf, f32 = jnp.bfloat16, jnp.float32
        dma = pltpu.SemaphoreType.DMA
        scratch = [
            pltpu.VMEM((2, 2, tokens, d // 2), bf),
            pltpu.VMEM((3, tokens, W), bf),
            pltpu.VMEM((2, d // 2, W), f32),
            pltpu.VMEM((4, d // 2, W), bf),
            pltpu.VMEM((4, d // 2, W), bf),
            pltpu.VMEM((8, d // 4, W), bf),
            pltpu.VMEM((8, d // 4, W), bf),
            pltpu.VMEM((4, d // 4, W), f32),
            pltpu.VMEM((8, d // 8, W), bf),
            pltpu.VMEM((8, d // 8, W), bf),
            pltpu.VMEM((4, d // 8, W), f32),
            dma((2, 2)), dma((3,)), dma((4,)), dma((4,)), dma((8,)), dma((8,)), dma((8,)), dma((8,)),
            dma((rounds,)), dma((rounds,)), dma((rounds,)), dma, dma,
        ]
        t = pl.pallas_call(
            kernel,
            out_shape=pltpu.VMEM((mats, d, ff), bf),
            in_specs=[pl.BlockSpec(memory_space=pl.ANY)] * 2,
            out_specs=pl.BlockSpec(memory_space=pltpu.VMEM),
            scratch_shapes=scratch,
            compiler_params=pltpu.CompilerParams(collective_id=0, has_side_effects=True, vmem_limit_bytes=34 << 20),
            name="sums",
        )(a, g)
        return pl.pallas_call(
            put,
            out_shape=jax.ShapeDtypeStruct((mats, d, ff), bf),
            in_specs=[pl.BlockSpec(memory_space=pltpu.VMEM)],
            out_specs=pl.BlockSpec(memory_space=pl.ANY),
            scratch_shapes=[dma((mats,))],
            compiler_params=pltpu.CompilerParams(vmem_limit_bytes=4 << 20),
            name="put",
        )(t)

    return jax.shard_map(step, mesh=mesh, in_specs=(P(("rep", "dp")), P(("rep", "dp"))), out_specs=P("rep"),
                         check_vma=False)
```

time: 763 us -> 252 us (0.33)
  blocking collectives: 634 us -> 0 us
  Pallas kernels: 0 us -> 252 us
  matrix products: 130 us -> 0 us
    dot_general x1 -> x0, blocking collectives: 634 us -> none  [step(): jnp.einsum('rsntd,rsntf->rndf', a, g, preferred_element_type=jnp.float32)]
    pallas_call x0 -> x2, Pallas kernels: none -> 252 us  [the longest x1 243 us: step(): pl.pallas_call(kernel, out_shape=pltpu.VMEM((mats, d, ff), bf), in_specs=...]
    dot_general x1 -> x0, matrix products: 130 us -> none  [step(): jnp.einsum('rsntd,rsntf->rndf', a, g, preferred_element_type=jnp.float32)]
where the time goes in v2:
time: 252 us
  Pallas kernels  252 us (100%)
    pallas_call x1, Pallas kernels, step(): pl.pallas_call(kernel, out_shape=pltpu.VMEM((mats, d, ff), bf), in_specs=...  243 us
    pallas_call x1, Pallas kernels, step(): pl.pallas_call(put, out_shape=jax.ShapeDtypeStruct((mats, d, ff), bf), in...  9.25 us

profile of v2, /device:TPU:0, one launch (start us, length us, event | category | flops | bytes accessed | tf_op | source)
XLA Modules:
  0.0 251.9 jit_solution(5582805740408126421)
XLA Ops:
  0.0 242.7 %sums.1.t_ref = bf16[4,1024,3328]{2,1,0:T(8,128)(2,1)S(1)} custom-call(bf16[1,4,4096,1024]{3,2,1,0:T(8,128)(2,1)} %a_ref.1, bf16[1,4,4096,3328]{3,2,1,0:T(8,128)(2,1)} %g_ref.1), custom_call_target="tpu_custom_call" | custom-call | tf_op jit(solution)/shard_map/sums/pallas_call | solution.py:255
  242.7 9.3 %put.1 = bf16[4,1024,3328]{2,1,0:T(8,128)(2,1)} custom-call(bf16[4,1024,3328]{2,1,0:T(8,128)(2,1)S(1)} %sums.1.t_ref), custom_call_target="tpu_custom_call" | custom-call | tf_op jit(solution)/shard_map/put/pallas_call | solution.py:264

commit v3 on v2

--- a/solution.py
+++ b/solution.py
@@ -8,7 +8,8 @@
 MESH = pl.DeviceIdType.MESH
 W = 256
 LAG1, LAG2, LAG3 = 1, 3, 5
-AG_START, AG_EVERY = 7, 1
+AG_START, AG_SKIP = 5, 2
+AGL2, AGL3 = 2, 4
 
 
 def kernel(a_ref, g_ref, t_ref, a_in, g_in, mine, d2d_out, d2d_got, rs1_out, rs1_got, keep1,
@@ -112,19 +113,20 @@
         return q if p is True else p & q
 
     def spread(r):
-        s = (r - AG_START) // AG_EVERY
-
-        @pl.when((r >= AG_START) & ((r - AG_START) % AG_EVERY == 0))
+        u = r - AG_START
+        s = u - u // AG_SKIP
+
+        @pl.when((u >= 0) & (u % AG_SKIP != AG_SKIP - 1))
         def _():
             spread1(s)
 
-            @pl.when(s >= 1)
-            def _():
-                spread2(s - 1)
-
-            @pl.when(s >= 2)
-            def _():
-                spread3(s - 2)
+            @pl.when(s >= AGL2)
+            def _():
+                spread2(s - AGL2)
+
+            @pl.when(s >= AGL3)
+            def _():
+                spread3(s - AGL3)
 
     def round_(r, first=False, compute=True, one=True, two=True, three=True, reuse=True):
         if compute:
@@ -161,17 +163,26 @@
                 def _():
                     a_side(0, own).wait()
 
-        when(one, lambda: d2d(r - LAG1).wait_recv())
+        if not first:
+            when(one, lambda: d2d(r - LAG1).wait_recv())
         when(two, lambda: rs1(r - LAG2).wait_recv())
         when(three, lambda: rs2(r - LAG3).wait_recv())
-        when(both(one, r - LAG1 >= 8), lambda: rs1(r - LAG1 - 8).wait_send())
+        if not first:
+            when(both(one, r - LAG1 >= 8), lambda: rs1(r - LAG1 - 8).wait_send())
         when(both(two, r - LAG2 >= 8), lambda: rs2(r - LAG2 - 8).wait_send())
-        when(one, lambda: combine(r - LAG1))
-        when(one, lambda: rs1(r - LAG1).start())
+        if not first:
+            when(one, lambda: combine(r - LAG1))
+            when(one, lambda: rs1(r - LAG1).start())
         when(two, lambda: stage2(r - LAG2))
         when(two, lambda: rs2(r - LAG2).start())
         if compute:
             mine[r % 2] = dot(r, own)
+        if first:
+            @pl.when(r < LAG3 - LAG1)
+            def _():
+                d2d(r).wait_recv()
+                combine(r)
+                rs1(r).start()
         when(three, lambda: stage3(r - LAG3))
         spread(r)
 
@@ -187,7 +198,7 @@
 
     @pl.loop(0, LAG3)
     def _(r):
-        round_(r, first=True, one=r >= LAG1, two=r >= LAG2, three=False)
+        round_(r, first=True, two=r >= LAG2, three=False)
 
     @pl.loop(LAG3, rounds)
     def _(r):
@@ -197,19 +208,20 @@
     def _(r):
         round_(r, compute=False, one=r < rounds + LAG1, two=r < rounds + LAG2)
 
-    done = -(-(rounds + LAG3 - AG_START) // AG_EVERY)
+    turns = rounds + LAG3 - AG_START
+    done = turns - turns // AG_SKIP
 
     @pl.loop(done, rounds)
     def _(s):
         spread1(s)
 
-    @pl.loop(done - 1, rounds + 1)
+    @pl.loop(done - AGL2, rounds)
     def _(s):
-        @pl.when(s < rounds)
-        def _():
-            spread2(s)
-
-        spread3(s - 1)
+        spread2(s)
+
+    @pl.loop(done - AGL3, rounds)
+    def _(s):
+        spread3(s)
 
     for k in range(4):
         d2d(rounds - 4 + k).wait_send()
@@ -223,7 +235,9 @@
 
 
 def put(t_ref, o_ref, sem):
-    copies = [pltpu.make_async_copy(t_ref.at[n], o_ref.at[n], sem.at[n]) for n in range(t_ref.shape[0])]
+    rows = t_ref.shape[1] // 4
+    copies = [pltpu.make_async_copy(t_ref.at[n, pl.ds(k * rows, rows)], o_ref.at[n, pl.ds(k * rows, rows)], sem.at[n, k])
+              for n in range(t_ref.shape[0]) for k in range(4)]
     for copy in copies:
         copy.start()
     for copy in copies:
@@ -266,7 +280,7 @@
             out_shape=jax.ShapeDtypeStruct((mats, d, ff), bf),
             in_specs=[pl.BlockSpec(memory_space=pltpu.VMEM)],
             out_specs=pl.BlockSpec(memory_space=pl.ANY),
-            scratch_shapes=[dma((mats,))],
+            scratch_shapes=[dma((mats, 4))],
             compiler_params=pltpu.CompilerParams(vmem_limit_bytes=4 << 20),
             name="put",
         )(t)

time: 252 us -> 247 us (0.980)
  Pallas kernels: 252 us -> 247 us
    pallas_call x1, Pallas kernels: 243 us -> 238 us  [step(): pl.pallas_call(kernel, out_shape=pltpu.VMEM((mats, d, ff), bf), in_specs=...]
where the time goes in v3:
time: 247 us
  Pallas kernels  247 us (100%)
    pallas_call x1, Pallas kernels, step(): pl.pallas_call(kernel, out_shape=pltpu.VMEM((mats, d, ff), bf), in_specs=...  238 us
    pallas_call x1, Pallas kernels, step(): pl.pallas_call(put, out_shape=jax.ShapeDtypeStruct((mats, d, ff), bf), in...  9.16 us

profile of v3, /device:TPU:0, one launch (start us, length us, event | category | flops | bytes accessed | tf_op | source)
XLA Modules:
  0.0 247.2 jit_solution(17981390844527307302)
XLA Ops:
  0.0 238.0 %sums.1.t_ref = bf16[4,1024,3328]{2,1,0:T(8,128)(2,1)S(1)} custom-call(bf16[1,4,4096,1024]{3,2,1,0:T(8,128)(2,1)} %a_ref.1, bf16[1,4,4096,3328]{3,2,1,0:T(8,128)(2,1)} %g_ref.1), custom_call_target="tpu_custom_call" | custom-call | tf_op jit(solution)/shard_map/sums/pallas_call | solution.py:269
  238.0 9.2 %put.1 = bf16[4,1024,3328]{2,1,0:T(8,128)(2,1)} custom-call(bf16[4,1024,3328]{2,1,0:T(8,128)(2,1)S(1)} %sums.1.t_ref), custom_call_target="tpu_custom_call" | custom-call | tf_op jit(solution)/shard_map/put/pallas_call | solution.py:278

commit v4 on v3

--- a/solution.py
+++ b/solution.py
@@ -7,8 +7,8 @@
 
 MESH = pl.DeviceIdType.MESH
 W = 256
-LAG1, LAG2, LAG3 = 1, 3, 5
-AG_START, AG_SKIP = 5, 2
+RAMP, LAG2, LAG3 = 8, 3, 5
+AG_START, AG_SKIP = 4, 4
 AGL2, AGL3 = 2, 4
 
 
@@ -128,7 +128,7 @@
             def _():
                 spread3(s - AGL3)
 
-    def round_(r, first=False, compute=True, one=True, two=True, three=True, reuse=True):
+    def round_(r, lag2, lag3, first=False, compute=True, two=True, three=True):
         if compute:
             n, j = r // nb, r % nb
 
@@ -163,50 +163,43 @@
                 def _():
                     a_side(0, own).wait()
 
-        if not first:
-            when(one, lambda: d2d(r - LAG1).wait_recv())
-        when(two, lambda: rs1(r - LAG2).wait_recv())
-        when(three, lambda: rs2(r - LAG3).wait_recv())
-        if not first:
-            when(both(one, r - LAG1 >= 8), lambda: rs1(r - LAG1 - 8).wait_send())
-        when(both(two, r - LAG2 >= 8), lambda: rs2(r - LAG2 - 8).wait_send())
-        if not first:
-            when(one, lambda: combine(r - LAG1))
-            when(one, lambda: rs1(r - LAG1).start())
-        when(two, lambda: stage2(r - LAG2))
-        when(two, lambda: rs2(r - LAG2).start())
+        when(two, lambda: rs1(r - lag2).wait_recv())
+        when(three, lambda: rs2(r - lag3).wait_recv())
+        when(both(two, r - lag2 >= 8), lambda: rs2(r - lag2 - 8).wait_send())
+        when(two, lambda: stage2(r - lag2))
+        when(two, lambda: rs2(r - lag2).start())
         if compute:
             mine[r % 2] = dot(r, own)
-        if first:
-            @pl.when(r < LAG3 - LAG1)
-            def _():
-                d2d(r).wait_recv()
-                combine(r)
-                rs1(r).start()
-        when(three, lambda: stage3(r - LAG3))
+        when(three, lambda: stage3(r - lag3))
+        if compute:
+            when(r >= 8, lambda: rs1(r - 8).wait_send())
+            d2d(r).wait_recv()
+            combine(r)
+            rs1(r).start()
         spread(r)
 
     a_side(0, other).start()
     g_copy(0).start()
-    a_side(0, own).start()
-    g_copy(1).start()
 
     barrier = pltpu.get_barrier_semaphore()
     for dev in (sib, to_a, to_b):
         pl.semaphore_signal(barrier, inc=1, device_id={"dp": dev}, device_id_type=MESH)
     pl.semaphore_wait(barrier, 3)
 
-    @pl.loop(0, LAG3)
+    a_side(0, own).start()
+    g_copy(1).start()
+
+    @pl.loop(0, RAMP)
     def _(r):
-        round_(r, first=True, two=r >= LAG2, three=False)
-
-    @pl.loop(LAG3, rounds)
+        round_(r, 2, 3, first=True, two=(r >= 2) & (r - 2 < RAMP - LAG2), three=(r >= 3) & (r - 3 < RAMP - LAG3))
+
+    @pl.loop(RAMP, rounds)
     def _(r):
-        round_(r)
+        round_(r, LAG2, LAG3)
 
     @pl.loop(rounds, rounds + LAG3)
     def _(r):
-        round_(r, compute=False, one=r < rounds + LAG1, two=r < rounds + LAG2)
+        round_(r, LAG2, LAG3, compute=False, two=r < rounds + LAG2)
 
     turns = rounds + LAG3 - AG_START
     done = turns - turns // AG_SKIP

time: 247 us -> 246 us (level)
  no operation moved by 1% of the time
where the time goes in v4:
time: 246 us
  Pallas kernels  246 us (100%)
    pallas_call x1, Pallas kernels, step(): pl.pallas_call(kernel, out_shape=pltpu.VMEM((mats, d, ff), bf), in_specs=...  237 us
    pallas_call x1, Pallas kernels, step(): pl.pallas_call(put, out_shape=jax.ShapeDtypeStruct((mats, d, ff), bf), in...  9.16 us

profile of v4, /device:TPU:0, one launch (start us, length us, event | category | flops | bytes accessed | tf_op | source)
XLA Modules:
  0.0 246.4 jit_solution(17250588390686075484)
XLA Ops:
  0.0 237.2 %sums.1.t_ref = bf16[4,1024,3328]{2,1,0:T(8,128)(2,1)S(1)} custom-call(bf16[1,4,4096,1024]{3,2,1,0:T(8,128)(2,1)} %a_ref.1, bf16[1,4,4096,3328]{3,2,1,0:T(8,128)(2,1)} %g_ref.1), custom_call_target="tpu_custom_call" | custom-call | tf_op jit(solution)/shard_map/sums/pallas_call | solution.py:262
  237.2 9.2 %put.1 = bf16[4,1024,3328]{2,1,0:T(8,128)(2,1)} custom-call(bf16[4,1024,3328]{2,1,0:T(8,128)(2,1)S(1)} %sums.1.t_ref), custom_call_target="tpu_custom_call" | custom-call | tf_op jit(solution)/shard_map/put/pallas_call | solution.py:271

commit v5 on v4

--- a/solution.py
+++ b/solution.py
@@ -14,7 +14,7 @@
 
 def kernel(a_ref, g_ref, t_ref, a_in, g_in, mine, d2d_out, d2d_got, rs1_out, rs1_got, keep1,
            rs2_out, rs2_got, keep2,
-           a_sem, g_sem, d2d_s, d2d_r, rs1_s, rs1_r, rs2_s, rs2_r, ag1_r, ag2a_r, ag2b_r, sib_r, ag_s):
+           h_sem, a_sem, g_sem, d2d_s, d2d_r, rs1_s, rs1_r, rs2_s, rs2_r, ag1_r, ag2a_r, ag2b_r, sib_r, ag_s):
     mats, tokens, d = a_ref.shape[1:]
     ff = g_ref.shape[3]
     nb = ff // W
@@ -67,6 +67,19 @@
         return lax.dot_general(a_in[(r // nb) % 2, side // half_d], g_in[r % 3],
                                (((0,), (0,)), ((), ())), preferred_element_type=f32)
 
+    def head(k):
+        rows = pl.ds(tokens // 2 * k, tokens // 2)
+        cols = pl.ds(pl.multiple_of(other, half_d), half_d)
+        return (pltpu.make_async_copy(a_ref.at[0, 0, rows, cols], a_in.at[0, other // half_d, rows], h_sem.at[k, 0]),
+                pltpu.make_async_copy(g_ref.at[0, 0, rows, pl.ds(0, W)], g_in.at[0, rows], h_sem.at[k, 1]))
+
+    def head_dot(k):
+        for copy in head(k):
+            copy.wait()
+        rows = pl.ds(tokens // 2 * k, tokens // 2)
+        return lax.dot_general(a_in[0, other // half_d, rows], g_in[0, rows], (((0,), (0,)), ((), ())),
+                               preferred_element_type=f32)
+
     def combine(r):
         lo, up = pl.multiple_of(h * (1 - pa), h), pl.multiple_of(h * pa, h)
         rs1_out[r % 8] = (mine[r % 2, pl.ds(lo, h)] + d2d_got[r % 4, pl.ds(lo, h)].astype(f32)).astype(bf)
@@ -142,18 +155,23 @@
                 for i in range(2):
                     a_copy(n, i).wait()
 
-            g_copy(r).wait()
+            when(r > 0 if first else True, lambda: g_copy(r).wait())
 
             @pl.when(r + 2 < rounds)
             def _():
                 g_copy(r + 2).start()
 
+            when((r >= 4) if first else True, lambda: d2d(r - 4).wait_send())
             if first:
                 @pl.when(r == 0)
                 def _():
-                    a_side(0, other).wait()
-            when((r >= 4) if first else True, lambda: d2d(r - 4).wait_send())
-            @pl.when(me >= 0)
+                    mine[1] = head_dot(0)
+
+                @pl.when((r == 0) & (me >= 0))
+                def _():
+                    d2d_out[0] = (mine[1] + head_dot(1)).astype(bf)
+
+            @pl.when((r > 0) if first else (me >= 0))
             def _():
                 d2d_out[r % 4] = dot(r, other).astype(bf)
 
@@ -178,8 +196,9 @@
             rs1(r).start()
         spread(r)
 
-    a_side(0, other).start()
-    g_copy(0).start()
+    for k in range(2):
+        for copy in head(k):
+            copy.start()
 
     barrier = pltpu.get_barrier_semaphore()
     for dev in (sib, to_a, to_b):
@@ -256,7 +275,7 @@
             pltpu.VMEM((8, d // 8, W), bf),
             pltpu.VMEM((8, d // 8, W), bf),
             pltpu.VMEM((4, d // 8, W), f32),
-            dma((2, 2)), dma((3,)), dma((4,)), dma((4,)), dma((8,)), dma((8,)), dma((8,)), dma((8,)),
+            dma((2, 2)), dma((2, 2)), dma((3,)), dma((4,)), dma((4,)), dma((8,)), dma((8,)), dma((8,)), dma((8,)),
             dma((rounds,)), dma((rounds,)), dma((rounds,)), dma, dma,
         ]
         t = pl.pallas_call(

time: 246 us -> 247 us (level)
  no operation moved by 1% of the time
where the time goes in v5:
time: 247 us
  Pallas kernels  246 us (100%)
    pallas_call x1, Pallas kernels, step(): pl.pallas_call(kernel, out_shape=pltpu.VMEM((mats, d, ff), bf), in_specs=...  237 us
    pallas_call x1, Pallas kernels, step(): pl.pallas_call(put, out_shape=jax.ShapeDtypeStruct((mats, d, ff), bf), in...  9.16 us

profile of v5, /device:TPU:0, one launch (start us, length us, event | category | flops | bytes accessed | tf_op | source)
XLA Modules:
  0.0 246.5 jit_solution(10274107357114615668)
XLA Ops:
  0.0 237.3 %sums.1.t_ref = bf16[4,1024,3328]{2,1,0:T(8,128)(2,1)S(1)} custom-call(bf16[1,4,4096,1024]{3,2,1,0:T(8,128)(2,1)} %a_ref.1, bf16[1,4,4096,3328]{3,2,1,0:T(8,128)(2,1)} %g_ref.1), custom_call_target="tpu_custom_call" | custom-call | tf_op jit(solution)/shard_map/sums/pallas_call | solution.py:281
  237.3 9.2 %put.1 = bf16[4,1024,3328]{2,1,0:T(8,128)(2,1)} custom-call(bf16[4,1024,3328]{2,1,0:T(8,128)(2,1)S(1)} %sums.1.t_ref), custom_call_target="tpu_custom_call" | custom-call | tf_op jit(solution)/shard_map/put/pallas_call | solution.py:290
